TPU v7x, 32 devices: a whole 2x2x4 slice. The times are simulated.
32 devices in a mesh: groups: 2 (over y), ep: 4 (over z), sub: 4 (over x, core).
Axes of the slice: x: 2, y: 2, z: 4, core: 2. Of those that a mesh axis runs over, the one named last changes fastest.
Arguments:
- tokens: bfloat16 [512, 7168], P(('groups', 'ep'), 'sub'), parts along dimension 0, may hold values from -6 to 6
- expert_ids: int32 [512, 2], P(('groups', 'ep')), parts along dimension 0, may hold values from 0 to 3, all different within a row; in each aligned block of 64 rows (0 to 63, 64 to 127, ...) at most 48 rows name the same one
- route_weights: float32 [512, 2], P(('groups', 'ep')), parts along dimension 0, may hold values from 0.05 to 0.6
- gate_weight: bfloat16 [4, 7168, 1024], P('ep', 'sub'), may hold values from -0.0625 to 0.0625
- up_weight: bfloat16 [4, 7168, 1024], P('ep', 'sub'), may hold values from -0.0625 to 0.0625
- down_weight: bfloat16 [4, 1024, 7168], P('ep', None, 'sub'), may hold values from -0.1875 to 0.1875
- shared_gate: bfloat16 [1024, 7168], P('ep', 'sub'), may hold values from -0.0625 to 0.0625
- shared_up: bfloat16 [1024, 7168], P('ep', 'sub'), may hold values from -0.0625 to 0.0625
- shared_down: bfloat16 [1024, 7168], P('ep', 'sub'), may hold values from -0.1875 to 0.1875
Outputs:
- layer_out: bfloat16 [512, 7168], P(('groups', 'ep'), 'sub'), parts along dimension 0
There are 2 independent parts, one for each index of `groups`. A program takes and returns all parts, laid end to end along the dimension named above; an argument that names none is the same for every part. Nothing has to cross between parts.
Inputs may be any that keep to these rules, and one draw needn't show every extreme that they name: `expert_ids`: each row names 2 different experts. Among the 64 rows of one ep index no expert is named more than 48 times, and in some of these aligned blocks an expert is named exactly 48 times.
All inputs are finite; a program needn't handle non-finite values.
Results may differ from a plain program's by a relative error of at most 0.0054.
Values may be sent and summed in bfloat16 or wider, within the bound.
A program may use at most 128 MiB of HBM per device.

v0:
```python
import functools

import jax
import jax.numpy as jnp
from jax import lax
from jax.experimental import pallas as pl
from jax.experimental.pallas import tpu as pltpu
from jax.sharding import PartitionSpec as P

MESH = pl.DeviceIdType.MESH
F32 = jnp.float32
BF16 = jnp.bfloat16
NT = (((1,), (1,)), ((), ()))
TN = (((0,), (0,)), ((), ()))


def dot(a, b, dims=None):
    if dims is None:
        return jnp.dot(a, b, preferred_element_type=F32)
    return lax.dot_general(a, b, dims, preferred_element_type=F32)


def mirrored(me, step, count):
    total, bit = 0, 1
    while bit < count:
        total = total + ((me // bit + step // bit) % 2) * bit
        bit *= 2
    return total


def silu(v):
    return v / (1.0 + jnp.exp(-v))


def kernel(
    n, ns, top, tok, meta, gw, uw, dw, sg, su, sd, out,
    toks, metas, gv, uv, dv, sgv, suv, sdv,
    hp, hr, sp, sr, own, hidr, hids, place, wslot, cs, cr, acc,
    w_sem, tok_ss, tok_rs, meta_ss, meta_rs, hp_ss, hp_rs, sp_ss, sp_rs,
    hr_ss, hr_rs, hs_ss, hs_rs, cs_ss, cs_rs, fw_ss,
):
    me, mq = lax.axis_index("ep"), lax.axis_index("sub")
    rows, width = tok.shape
    slots = place.shape[1]
    piece = hp.shape[-1]
    part = sp.shape[-2]
    chunk = 256 if width % 256 == 0 else 128

    line = n == 4
    inner = ((me + 1) // 2) % 2 if line else me * 0

    def turn(i):
        return lax.rem(i + inner, n)

    weights = [
        pltpu.make_async_copy(src, dst, w_sem.at[i])
        for i, (src, dst) in enumerate(
            [(sg, sgv), (su, suv), (gw.at[0], gv), (uw.at[0], uv), (sd, sdv), (dw.at[0], dv)]
        )
    ]
    for copy in weights:
        copy.start()

    def peer(d):
        return lax.rem(mq + d, ns)

    def partner(s):
        return mirrored(me, s, n)

    def remote(src, dst, ss, rs, where):
        return pltpu.make_async_remote_copy(
            src_ref=src, dst_ref=dst, send_sem=ss, recv_sem=rs,
            device_id=where, device_id_type=MESH,
        )

    def tok_copy(s):
        return remote(tok, toks.at[s], tok_ss.at[s], tok_rs.at[s], {"ep": partner(s)})

    def forward_copy():
        return remote(
            toks.at[2], toks.at[3], fw_ss.at[0], tok_rs.at[3], {"ep": partner(1)}
        )

    def meta_copy(s):
        return remote(meta, metas.at[s], meta_ss.at[s], meta_rs.at[s], {"ep": partner(s)})

    def hp_copy(s, d):
        return remote(
            hp.at[s, d - 1], hr.at[s, d - 1], hp_ss.at[s, d - 1], hp_rs.at[s, d - 1],
            {"sub": peer(d)},
        )

    def sp_copy(s, d):
        return remote(
            sp.at[s, peer(d)], sr.at[s, d - 1], sp_ss.at[s, d - 1], sp_rs.at[s, d - 1],
            {"sub": peer(d)},
        )

    def hr_copy(s, d):
        return remote(
            hidr.at[s, mq], hidr.at[s, mq], hr_ss.at[s, d - 1], hr_rs.at[s, d - 1],
            {"sub": peer(d)},
        )

    def hs_copy(s, d):
        return remote(
            hids.at[s, mq], hids.at[s, mq], hs_ss.at[s, d - 1], hs_rs.at[s, d - 1],
            {"sub": peer(d)},
        )

    def cs_copy(s):
        return remote(cs.at[s], cr.at[s], cs_ss.at[s], cs_rs.at[s], {"ep": partner(s)})

    def loop(first, last, body):
        if last - first <= 8:
            for s in range(first, last):
                body(s)
        else:
            lax.fori_loop(first, last, lambda s, c: (body(s), c)[1], 0)

    barrier = pltpu.get_barrier_semaphore()
    loop(1, n, lambda s: pl.semaphore_signal(
        barrier, inc=1, device_id={"ep": partner(s)}, device_id_type=MESH))
    for d in range(1, ns):
        pl.semaphore_signal(barrier, inc=1, device_id={"sub": peer(d)}, device_id_type=MESH)
    pl.semaphore_wait(barrier, n - 1 + ns - 1)

    def send_tokens(s):
        meta_copy(s).start()
        if line and s == 3:
            pl.when(inner == 1)(lambda: tok_copy(s).start())
        else:
            tok_copy(s).start()

    loop(1, n, send_tokens)
    toks[0] = tok[...]
    metas[0] = meta[...]

    def project(i):
        s = turn(i)

        @pl.when(s > 0)
        def _():
            meta_copy(s).wait_recv()
            tok_copy(s).wait_recv()

        if line and isinstance(i, int) and i == 1:
            pl.when(inner == 1)(lambda: forward_copy().start())
        first = isinstance(i, int) and i == 0
        if first:
            for copy in weights[:2]:
                copy.wait()
        block, info = toks.at[s], metas[s]
        gate = dot(block[...], sgv[...], NT)
        sp[i, :, 0] = gate.astype(BF16).reshape(ns, part, -1)
        up = dot(block[...], suv[...], NT)
        sp[i, :, 1] = up.astype(BF16).reshape(ns, part, -1)
        for d in range(1, ns):
            sp_copy(i, d).start()

        hit = (info[:top, :rows] == me.astype(F32)).astype(F32)
        member = jnp.sum(hit, axis=0, keepdims=True)
        weight = jnp.sum(hit * info[top:2 * top, :rows], axis=0, keepdims=True)
        before = (
            lax.broadcasted_iota(jnp.int32, (rows, rows), 0)
            < lax.broadcasted_iota(jnp.int32, (rows, rows), 1)
        ).astype(F32).astype(BF16)
        rank = dot(jnp.broadcast_to(member, (16, rows)).astype(BF16), before)[:1]
        spot = lax.broadcasted_iota(jnp.int32, (slots, rows), 0).astype(F32)
        placing = (spot == rank).astype(F32) * member
        wslot[i] = jnp.sum(placing * weight, axis=1, keepdims=True)
        placing = placing.astype(BF16)
        place[i] = placing
        picked = dot(placing, block[...]).astype(BF16)
        if first:
            for copy in weights[2:4]:
                copy.wait()
        for d in list(range(1, ns)) + [0]:
            cols = pl.ds(pl.multiple_of(peer(d) * piece, piece), piece)
            gate = dot(picked, gv[:, cols])
            up = dot(picked, uv[:, cols])
            if d:
                hp[i, d - 1, 0] = gate.astype(BF16)
                hp[i, d - 1, 1] = up.astype(BF16)
                hp_copy(i, d).start()
            else:
                own[i, 0] = gate
                own[i, 1] = up

    def activate(i):
        pre, lin = sp[i, mq, 0].astype(F32), sp[i, mq, 1].astype(F32)
        for d in range(1, ns):
            sp_copy(i, d).wait_recv()
            pre = pre + sr[i, d - 1, 0].astype(F32)
            lin = lin + sr[i, d - 1, 1].astype(F32)
        hids[i, mq] = (silu(pre) * lin).astype(BF16)
        for d in range(1, ns):
            hs_copy(i, d).start()
        pre, lin = own[i, 0], own[i, 1]
        for d in range(1, ns):
            hp_copy(i, d).wait_recv()
            pre = pre + hr[i, d - 1, 0].astype(F32)
            lin = lin + hr[i, d - 1, 1].astype(F32)
        hidr[i, mq] = (silu(pre) * lin).astype(BF16)
        for d in range(1, ns):
            hr_copy(i, d).start()

    def finish(i):
        s = turn(i)
        if isinstance(i, int) and i == 0:
            for copy in weights[4:]:
                copy.wait()
        for d in range(1, ns):
            hs_copy(i, d).wait_recv()
            hr_copy(i, d).wait_recv()
        hidden = jnp.concatenate([hidr[i, q] for q in range(ns)], axis=1)
        shared = hids[i].reshape(rows, -1)
        placing = place[i]
        scale = wslot[i]

        def columns(c, carry):
            cols = pl.ds(pl.multiple_of(c * chunk, chunk), chunk)
            routed = (dot(hidden, dv[:, cols]) * scale).astype(BF16)
            total = dot(placing, routed, TN) + dot(shared, sdv[:, cols])

            @pl.when(s == 0)
            def _():
                acc[:, cols] = total

            @pl.when(s > 0)
            def _():
                cs[s, :, cols] = total.astype(BF16)

            return carry

        lax.fori_loop(0, width // chunk, columns, 0)
        pl.when(s > 0)(lambda: cs_copy(s).start())

    project(0)
    activate(0)
    project(1)
    finish(0)
    activate(1)

    def step(s):
        project(s)
        finish(s - 1)
        activate(s)

    loop(2, n, step)
    finish(n - 1)

    def collect(s):
        cs_copy(s).wait_recv()
        acc[...] += cr[s].astype(F32)

    loop(1, n, collect)
    out[...] = acc[...].astype(out.dtype)

    def drain(s):
        if line and s == 3:
            @pl.when(inner == 1)
            def _():
                tok_copy(s).wait_send()
                forward_copy().wait_send()
        else:
            tok_copy(s).wait_send()
        meta_copy(s).wait_send()
        cs_copy(s).wait_send()

    loop(1, n, drain)

    def drain_sub(s):
        for d in range(1, ns):
            hp_copy(s, d).wait_send()
            sp_copy(s, d).wait_send()
            hr_copy(s, d).wait_send()
            hs_copy(s, d).wait_send()

    loop(0, n, drain_sub)


def per_device(tokens, expert_ids, route_weights, gate_weight, up_weight, down_weight,
               shared_gate, shared_up, shared_down):
    n, ns = lax.axis_size("ep"), lax.axis_size("sub")
    rows, width = tokens.shape
    top = expert_ids.shape[1]
    hidden = gate_weight.shape[2]
    local = shared_gate.shape[0]
    capacity = rows * top * 3 // (2 * n)
    slots = -(-capacity // 16) * 16
    piece, part = hidden // ns, rows // ns
    meta = jnp.concatenate([expert_ids.astype(F32), route_weights], axis=1).T
    meta = jnp.pad(meta, ((0, -(2 * top) % 8), (0, -rows % 128)))
    dma = pltpu.SemaphoreType.DMA
    vmem = pl.BlockSpec(memory_space=pltpu.VMEM)
    hbm = pl.BlockSpec(memory_space=pl.ANY)
    return pl.pallas_call(
        functools.partial(kernel, n, ns, top),
        out_shape=jax.ShapeDtypeStruct((rows, width), BF16),
        in_specs=[vmem] * 2 + [hbm] * 6,
        out_specs=vmem,
        scratch_shapes=[
            pltpu.VMEM((n, rows, width), BF16),
            pltpu.VMEM((n,) + meta.shape, F32),
            pltpu.VMEM((width, hidden), BF16),
            pltpu.VMEM((width, hidden), BF16),
            pltpu.VMEM((hidden, width), BF16),
            pltpu.VMEM((local, width), BF16),
            pltpu.VMEM((local, width), BF16),
            pltpu.VMEM((local, width), BF16),
            pltpu.VMEM((n, ns - 1, 2, slots, piece), BF16),
            pltpu.VMEM((n, ns - 1, 2, slots, piece), BF16),
            pltpu.VMEM((n, ns, 2, part, local), BF16),
            pltpu.VMEM((n, ns - 1, 2, part, local), BF16),
            pltpu.VMEM((n, 2, slots, piece), F32),
            pltpu.VMEM((n, ns, slots, piece), BF16),
            pltpu.VMEM((n, ns, part, local), BF16),
            pltpu.VMEM((n, slots, rows), BF16),
            pltpu.VMEM((n, slots, 1), F32),
            pltpu.VMEM((n, rows, width), BF16),
            pltpu.VMEM((n, rows, width), BF16),
            pltpu.VMEM((rows, width), F32),
            dma((6,)),
            dma((n,)), dma((n,)), dma((n,)), dma((n,)),
            dma((n, ns - 1)), dma((n, ns - 1)), dma((n, ns - 1)), dma((n, ns - 1)),
            dma((n, ns - 1)), dma((n, ns - 1)), dma((n, ns - 1)), dma((n, ns - 1)),
            dma((n,)), dma((n,)), dma((1,)),
        ],
        compiler_params=pltpu.CompilerParams(collective_id=0, has_side_effects=True),
    )(tokens, meta, gate_weight, up_weight, down_weight, shared_gate, shared_up, shared_down)


def solution(mesh):
    in_specs = (
        P(("groups", "ep"), "sub"),
        P(("groups", "ep"), None),
        P(("groups", "ep"), None),
        P("ep", "sub", None),
        P("ep", "sub", None),
        P("ep", None, "sub"),
        P("ep", "sub"),
        P("ep", "sub"),
        P("ep", "sub"),
    )
    out_specs = P(("groups", "ep"), "sub")
    return jax.shard_map(
        per_device, mesh=mesh, in_specs=in_specs, out_specs=out_specs, check_vma=False
    )
```

profile of v0, /device:TPU:17, one launch (start us, length us, event | category | flops | bytes accessed | tf_op | source)
XLA Modules:
  0.0 56.1 jit_solution(841292017161162835)
XLA Ops:
  0.0 0.7 %convert_element_type.5 = f32[64,2]{0,1:T(2,128)S(1)} convert(s32[64,2]{0,1:T(2,128)} %param.10) | non-fusion elementwise | flops 128 | bytes 1024 | tf_op jit(solution)/shard_map/convert_element_type | solution.py:293
  0.7 0.7 %maximum_bitcast_fusion = f32[4,64]{1,0:T(4,128)S(1)} fusion(f32[64,2]{0,1:T(2,128)} %param.11, f32[64,2]{0,1:T(2,128)S(1)} %convert_element_type.5), kind=kLoop, calls=%fused_computation | loop fusion | flops 256 | bytes 2048 | tf_op jit(solution)/shard_map/transpose | solution.py:293
  1.4 0.6 %pad.4.meta = f32[8,128]{1,0:T(8,128)} pad(f32[4,64]{1,0:T(4,128)S(1)} %maximum_bitcast_fusion, f32[]{:T(128)} %constant.2.clone.1), padding=0_4x0_64 | pad | bytes 5124 | tf_op jit(solution)/shard_map/jit(_pad)/pad | solution.py:294
  2.0 52.5 %shard_map.91 = bf16[64,1792]{1,0:T(8,128)(2,1)} custom-call(bf16[64,1792]{1,0:T(8,128)(2,1)} %tok.1, f32[8,128]{1,0:T(8,128)} %pad.4.meta, bf16[1,1792,1024]{2,1,0:T(8,128)(2,1)} %gw.1, bf16[1,1792,1024]{2,1,0:T(8,128)(2,1)} %uw.1, bf16[1,1024,1792]{2,1,0:T(8,128)(2,1)} %dw.1, bf16[256,1792]{1,0:T(8,128)(2,1)} %sg.1, bf16[256,1792]{1,0:T(8,128)(2,1)} %su.1, ...), custom_call_target="tpu_custom_call" | custom-call | tf_op jit(solution)/shard_map/pallas_call | solution.py:298
  54.5 1.6 %copy.11 = bf16[64,1792]{1,0:T(8,128)(2,1)} copy(bf16[64,1792]{1,0:T(8,128)(2,1)} %shard_map.91) | data formatting | bytes 458752
where the time goes:
time: 56.3 us; the launch traced here: 56.1 us
  Pallas kernels  52.5 us (93%)
  local copies, waits for them, and re-layouts  2.24 us (4%)
  other arithmetic  1.37 us (2%)
    pallas_call x1, Pallas kernels, per_device(): pl.pallas_call(functools.partial(kernel, n, ns, top), out_shape=jax.Shape...  52.5 us
    unnamed x1, local copies, waits for them, and re-layouts  1.64 us

commit v1 on v0

--- a/solution.py
+++ b/solution.py
@@ -330,6 +330,300 @@
         compiler_params=pltpu.CompilerParams(collective_id=0, has_side_effects=True),
     )(tokens, meta, gate_weight, up_weight, down_weight, shared_gate, shared_up, shared_down)
 
+def line_kernel(
+    n, ns, top, tok, ids, rw, gw, uw, dw, sg, su, sd, acc, cr,
+    toks, metas, idv, rwv, gv, uv, dv, sguv, sdv, wcol, part, peer, own, xs, xr, hid, cs,
+    w_sem, in_sem, tok_ss, tok_rs, meta_ss, meta_rs, d_ss, d_rs, x_ss, x_rs, h_ss, h_rs,
+    c_ss, c_rs,
+):
+    me, mq = lax.axis_index("ep"), lax.axis_index("sub")
+    rows, width = tok.shape
+    half_rows = rows // 2
+    hh, ll = gv.shape[1] // 2, sguv.shape[1] // 2
+    chunk = 256 if width % 256 == 0 else 128
+    core = lax.rem(mq, 2)
+    mate = mq + 1 - 2 * core
+    across = lax.rem(mq + 2, ns)
+    sign = 1 - 2 * (me // 2)
+    inner = ((me + 1) // 2) % 2
+    source = [me, me + sign * (1 - 2 * inner), me + sign * (2 - inner), me + sign * (3 - inner)]
+    units = [(0, 0, rows), (1, 0, rows), (2, 0, rows), (3, 0, half_rows), (3, half_rows, half_rows)]
+    pieces = [pl.ds(0, hh), pl.ds(hh, hh), pl.ds(2 * hh, 2 * ll)]
+
+    def remote(src, dst, ss, rs, where):
+        return pltpu.make_async_remote_copy(
+            src_ref=src, dst_ref=dst, send_sem=ss, recv_sem=rs,
+            device_id=where, device_id_type=MESH,
+        )
+
+    def on_inner(body):
+        pl.when(inner == 1)(body)
+
+    def on_edge(body):
+        pl.when(inner == 0)(body)
+
+    inputs = [
+        pltpu.make_async_copy(tok, toks.at[me], in_sem.at[0]),
+        pltpu.make_async_copy(ids, idv, in_sem.at[1]),
+        pltpu.make_async_copy(rw, rwv, in_sem.at[2]),
+    ]
+    weights = [
+        pltpu.make_async_copy(gw.at[0], gv, w_sem.at[0]),
+        pltpu.make_async_copy(uw.at[0], uv, w_sem.at[1]),
+    ]
+    for h in range(2):
+        for j, src in enumerate((sg, su)):
+            weights.append(pltpu.make_async_copy(
+                src.at[pl.ds(h * ll, ll)], sguv.at[h, pl.ds(j * ll, ll)], w_sem.at[2 + 2 * h + j]))
+    weights.append(pltpu.make_async_copy(dw.at[0], dv, w_sem.at[6]))
+    weights.append(pltpu.make_async_copy(sd, sdv, w_sem.at[7]))
+    for copy in inputs + weights:
+        copy.start()
+
+    barrier = pltpu.get_barrier_semaphore()
+    pl.semaphore_signal(barrier, inc=1, device_id={"ep": me + sign}, device_id_type=MESH)
+    on_inner(lambda: pl.semaphore_signal(
+        barrier, inc=1, device_id={"ep": me - sign}, device_id_type=MESH))
+    pl.semaphore_signal(barrier, inc=1, device_id={"sub": mate}, device_id_type=MESH)
+    pl.semaphore_signal(barrier, inc=1, device_id={"sub": across}, device_id_type=MESH)
+    pl.semaphore_wait(barrier, 3 + inner)
+
+    def tok_copy(s, h, away):
+        block = toks.at[s, pl.ds(h * half_rows, half_rows)]
+        return remote(block, block, tok_ss.at[s, h, away], tok_rs.at[s, h],
+                      {"ep": me + sign * (1 - 2 * away)})
+
+    def meta_copy(s, away):
+        return remote(metas.at[s], metas.at[s], meta_ss.at[s, away], meta_rs.at[s],
+                      {"ep": me + sign * (1 - 2 * away)})
+
+    def mate_copy(u, j):
+        m = units[u][2]
+        return remote(part.at[u, pl.ds(0, m), pieces[j]], peer.at[u, pl.ds(0, m), pieces[j]],
+                      d_ss.at[u, j], d_rs.at[u, j], {"sub": mate})
+
+    def across_copy(u):
+        m = units[u][2]
+        return remote(xs.at[u, pl.ds(0, m)], xr.at[u, pl.ds(0, m)], x_ss.at[u], x_rs.at[u],
+                      {"sub": across})
+
+    def hid_copy(u):
+        block = hid.at[u, core, pl.ds(0, units[u][2])]
+        return remote(block, block, h_ss.at[u], h_rs.at[u], {"sub": mate})
+
+    def out_copy(k, h):
+        s, where = source[k], pl.ds(h * half_rows, half_rows)
+        slot = lax.rem(me - s + n, n) - 1
+        return remote(cs.at[k - 1, where], cr.at[slot, where], c_ss.at[k - 1, h],
+                      c_rs.at[slot, h], {"ep": s})
+
+    inputs[0].wait()
+    for h in range(2):
+        on_inner(lambda h=h: tok_copy(me, h, 1).start())
+        tok_copy(me, h, 0).start()
+    inputs[1].wait()
+    inputs[2].wait()
+    metas[me] = jnp.zeros(metas.shape[1:], F32)
+    for e in range(n):
+        metas[me, e:e + 1, :rows] = jnp.sum(
+            jnp.where(idv[...] == e, rwv[...], 0.0), axis=0, keepdims=True)
+    on_inner(lambda: meta_copy(me, 1).start())
+    meta_copy(me, 0).start()
+
+    def take(k, halves):
+        if 0 in halves:
+            meta_copy(source[k], 0).wait_recv()
+        for h in halves:
+            tok_copy(source[k], h, 0).wait_recv()
+
+    def forward(k, h, away):
+        s = source[k]
+        tok_copy(s, h, 0).wait_recv()
+        tok_copy(s, h, away).start()
+        if h == 0:
+            meta_copy(s, 0).wait_recv()
+            meta_copy(s, away).start()
+
+    def project(u):
+        k, first, m = units[u]
+        block = toks.at[source[k], pl.ds(first, m)]
+        mine = pl.ds(0, m)
+        for side, dst in ((1 - core, part), (core, own)):
+            cols = pl.ds(pl.multiple_of(side * hh, hh), hh)
+            dst[u, mine, pieces[0]] = dot(block[...], gv[:, cols])
+            if dst is part:
+                mate_copy(u, 0).start()
+            dst[u, mine, pieces[1]] = dot(block[...], uv[:, cols])
+            if dst is part:
+                mate_copy(u, 1).start()
+            dst[u, mine, pieces[2]] = dot(block[...], sguv[side], NT)
+            if dst is part:
+                mate_copy(u, 2).start()
+
+    def reduce(u):
+        mine = pl.ds(0, units[u][2])
+        for j, cols in enumerate(pieces):
+            mate_copy(u, j).wait_recv()
+            total = own[u, mine, cols] + peer[u, mine, cols]
+            own[u, mine, cols] = total
+            xs[u, mine, cols] = total.astype(BF16)
+        across_copy(u).start()
+
+    def activate(u):
+        mine = pl.ds(0, units[u][2])
+        across_copy(u).wait_recv()
+        gate, up, shared = [own[u, mine, cols] + xr[u, mine, cols].astype(F32) for cols in pieces]
+        hid[u, core, mine, pl.ds(0, hh)] = (silu(gate) * up).astype(BF16)
+        hid[u, core, mine, pl.ds(hh, ll)] = (silu(shared[:, :ll]) * shared[:, ll:]).astype(BF16)
+        hid_copy(u).start()
+
+    def weigh(k):
+        line = metas[source[k], pl.ds(me, 1), pl.ds(0, rows)]
+        eye = (
+            lax.broadcasted_iota(jnp.int32, (rows, rows), 0)
+            == lax.broadcasted_iota(jnp.int32, (rows, rows), 1)
+        )
+        wcol[k] = jnp.sum(jnp.where(eye, line, 0.0), axis=1, keepdims=True)
+
+    def finish(u):
+        k, first, m = units[u]
+        mine = pl.ds(0, m)
+        scale = wcol[k, pl.ds(first, m)]
+        hid_copy(u).wait_recv()
+        routed = jnp.concatenate([hid[u, c, mine, pl.ds(0, hh)] for c in range(2)], axis=1)
+        shared = jnp.concatenate([hid[u, c, mine, pl.ds(hh, ll)] for c in range(2)], axis=1)
+        for c in range(width // chunk):
+            cols = pl.ds(c * chunk, chunk)
+            total = dot(routed, dv[:, cols]) * scale + dot(shared, sdv[:, cols])
+            if k == 0:
+                acc[:, cols] = total
+            else:
+                cs[k - 1, pl.ds(first, m), cols] = total.astype(BF16)
+        if k:
+            for h in range(first // half_rows, (first + m) // half_rows):
+                out_copy(k, h).start()
+
+    for copy in weights[:6]:
+        copy.wait()
+    project(0)
+
+    @on_inner
+    def _():
+        forward(2, 0, 1)
+        forward(1, 0, 0)
+
+    weigh(0)
+    reduce(0)
+
+    @on_inner
+    def _():
+        forward(2, 1, 1)
+        forward(1, 1, 0)
+
+    on_edge(lambda: take(1, (0, 1)))
+    project(1)
+    weigh(1)
+    reduce(1)
+    on_inner(lambda: forward(3, 0, 1))
+    activate(0)
+    on_edge(lambda: take(2, (0, 1)))
+    project(2)
+    weigh(2)
+    on_inner(lambda: forward(3, 1, 1))
+    reduce(2)
+    for copy in weights[6:]:
+        copy.wait()
+    finish(0)
+    activate(1)
+    on_edge(lambda: take(3, (0,)))
+    project(3)
+    weigh(3)
+    reduce(3)
+    finish(1)
+    on_edge(lambda: take(3, (1,)))
+    project(4)
+    reduce(4)
+    activate(2)
+    finish(2)
+    activate(3)
+    finish(3)
+    activate(4)
+    finish(4)
+
+    for slot in range(n - 1):
+        for h in range(2):
+            where = pl.ds(h * half_rows, half_rows)
+            remote(cs.at[slot, where], cr.at[slot, where], c_ss.at[slot, h], c_rs.at[slot, h],
+                   {"ep": me + sign}).wait_recv()
+    for k in range(1, n):
+        for h in range(2):
+            out_copy(k, h).wait_send()
+    for u in range(len(units)):
+        for j in range(len(pieces)):
+            mate_copy(u, j).wait_send()
+        across_copy(u).wait_send()
+        hid_copy(u).wait_send()
+    for h in range(2):
+        tok_copy(me, h, 0).wait_send()
+    meta_copy(me, 0).wait_send()
+
+    @on_inner
+    def _():
+        meta_copy(me, 1).wait_send()
+        for k, away in ((1, 0), (2, 1), (3, 1)):
+            meta_copy(source[k], away).wait_send()
+            for h in range(2):
+                tok_copy(source[k], h, away).wait_send()
+        for h in range(2):
+            tok_copy(me, h, 1).wait_send()
+
+
+def line_device(tokens, expert_ids, route_weights, gate_weight, up_weight, down_weight,
+                shared_gate, shared_up, shared_down):
+    n, ns = lax.axis_size("ep"), lax.axis_size("sub")
+    rows, width = tokens.shape
+    top = expert_ids.shape[1]
+    hidden = gate_weight.shape[2]
+    local = shared_gate.shape[0]
+    both, units = hidden + local, 5
+    dma = pltpu.SemaphoreType.DMA
+    vmem = pl.BlockSpec(memory_space=pltpu.VMEM)
+    hbm = pl.BlockSpec(memory_space=pl.ANY)
+    total, sums = pl.pallas_call(
+        functools.partial(line_kernel, n, ns, top),
+        out_shape=(pltpu.VMEM((rows, width), F32), pltpu.VMEM((n - 1, rows, width), BF16)),
+        in_specs=[hbm] * 9,
+        out_specs=(vmem, vmem),
+        scratch_shapes=[
+            pltpu.VMEM((n, rows, width), BF16),
+            pltpu.VMEM((n, -(-n // 8) * 8, -(-rows // 128) * 128), F32),
+            pltpu.VMEM((top, rows), jnp.int32),
+            pltpu.VMEM((top, rows), F32),
+            pltpu.VMEM((width, hidden), BF16),
+            pltpu.VMEM((width, hidden), BF16),
+            pltpu.VMEM((hidden, width), BF16),
+            pltpu.VMEM((2, local, width), BF16),
+            pltpu.VMEM((local, width), BF16),
+            pltpu.VMEM((n, rows, 1), F32),
+            pltpu.VMEM((units, rows, both), F32),
+            pltpu.VMEM((units, rows, both), F32),
+            pltpu.VMEM((units, rows, both), F32),
+            pltpu.VMEM((units, rows, both), BF16),
+            pltpu.VMEM((units, rows, both), BF16),
+            pltpu.VMEM((units, 2, rows, both // 2), BF16),
+            pltpu.VMEM((n - 1, rows, width), BF16),
+            dma((8,)), dma((3,)),
+            dma((n, 2, 2)), dma((n, 2)), dma((n, 2)), dma((n,)),
+            dma((units, 3)), dma((units, 3)), dma((units,)), dma((units,)),
+            dma((units,)), dma((units,)), dma((n - 1, 2)), dma((n - 1, 2)),
+        ],
+        compiler_params=pltpu.CompilerParams(collective_id=0, has_side_effects=True),
+    )(tokens, expert_ids.T, route_weights.T, gate_weight, up_weight, down_weight,
+      shared_gate, shared_up, shared_down)
+    for slot in range(n - 1):
+        total = total + sums[slot].astype(F32)
+    return total.astype(BF16)
+
 
 def solution(mesh):
     in_specs = (
@@ -344,6 +638,7 @@
         P("ep", "sub"),
     )
     out_specs = P(("groups", "ep"), "sub")
+    line = mesh.shape["ep"] == 4 and mesh.shape["sub"] == 4
     return jax.shard_map(
-        per_device, mesh=mesh, in_specs=in_specs, out_specs=out_specs, check_vma=False
+        line_device if line else per_device, mesh=mesh, in_specs=in_specs, out_specs=out_specs, check_vma=False
     )

time: 56.3 us -> 55.1 us (0.979)
  the two profiles are of different devices: /device:TPU:17 before, /device:TPU:0 now
where the time goes in v1:
time: 55.1 us; the launch traced here: 55 us
  Pallas kernels  54.2 us (98%)
  other arithmetic  0.79 us (1%)
    pallas_call x1, Pallas kernels, line_device(): pl.pallas_call(functools.partial(line_kernel, n, ns, top), out_shape=(plt...  54.2 us

profile of v1, /device:TPU:0, one launch (start us, length us, event | category | flops | bytes accessed | tf_op | source)
XLA Modules:
  0.0 55.0 jit_solution(13304163941517745740)
XLA Ops:
  0.0 54.2 %shard_map.91 = (f32[64,1792]{1,0:T(8,128)S(1)}, bf16[3,64,1792]{2,1,0:T(8,128)(2,1)S(1)}) custom-call(bf16[64,1792]{1,0:T(8,128)(2,1)} %tok.1, s32[2,64]{1,0:T(2,128)} %bitcast.11, f32[2,64]{1,0:T(2,128)} %bitcast.12, bf16[1,1792,1024]{2,1,0:T(8,128)(2,1)} %gw.1, bf16[1,1792,1024]{2,1,0:T(8,128)(2,1)} %uw.1, bf16[1,1024,1792]{2,1,0:T(8,128)(2,1)} %dw.1, ...), custom_call_target="tpu_custom_call" | custom-call | tf_op jit(solution)/shard_map/pallas_call | solution.py:592
  54.2 0.8 %fusion = bf16[64,1792]{1,0:T(8,128)(2,1)} fusion(f32[64,1792]{1,0:T(8,128)S(1)} %get-tuple-element.7, bf16[3,64,1792]{2,1,0:T(8,128)(2,1)S(1)} %get-tuple-element.8), kind=kLoop, calls=%fused_computation.1 | loop fusion | flops 802816 | bytes 1376256 | tf_op jit(solution)/shard_map/convert_element_type | solution.py:625

commit v2 on v1

--- a/solution.py
+++ b/solution.py
@@ -332,23 +332,31 @@
 
 def line_kernel(
     n, ns, top, tok, ids, rw, gw, uw, dw, sg, su, sd, acc, cr,
-    toks, metas, idv, rwv, gv, uv, dv, sguv, sdv, wcol, part, peer, own, xs, xr, hid, cs,
+    toks, metas, idv, rwv, gv, uv, dv, sgv, suv, sdv, turned, part, peer, own, xs, xr, hid, cs,
     w_sem, in_sem, tok_ss, tok_rs, meta_ss, meta_rs, d_ss, d_rs, x_ss, x_rs, h_ss, h_rs,
     c_ss, c_rs,
 ):
     me, mq = lax.axis_index("ep"), lax.axis_index("sub")
     rows, width = tok.shape
-    half_rows = rows // 2
-    hh, ll = gv.shape[1] // 2, sguv.shape[1] // 2
+    half = rows // 2
+    hh, ll = gv.shape[1] // 2, sgv.shape[0] // 2
     chunk = 256 if width % 256 == 0 else 128
     core = lax.rem(mq, 2)
     mate = mq + 1 - 2 * core
     across = lax.rem(mq + 2, ns)
     sign = 1 - 2 * (me // 2)
     inner = ((me + 1) // 2) % 2
-    source = [me, me + sign * (1 - 2 * inner), me + sign * (2 - inner), me + sign * (3 - inner)]
-    units = [(0, 0, rows), (1, 0, rows), (2, 0, rows), (3, 0, half_rows), (3, half_rows, half_rows)]
+    steps = [0, 1, 1 - 2 * inner, 2 - inner, 2 - 3 * inner, 3 - inner, 3 - inner]
+    source = [me + sign * step for step in steps]
+    parity = [0, 0, 1 - inner, inner, 1, 0, 1]
+    size = [rows] + [half] * 6
     pieces = [pl.ds(0, hh), pl.ds(hh, hh), pl.ds(2 * hh, 2 * ll)]
+
+    def span(h):
+        return pl.ds(h * half if isinstance(h, int) else pl.multiple_of(h * half, half), half)
+
+    def place(u):
+        return pl.ds(0, rows) if u == 0 else span(parity[u])
 
     def remote(src, dst, ss, rs, where):
         return pltpu.make_async_remote_copy(
@@ -368,16 +376,12 @@
         pltpu.make_async_copy(rw, rwv, in_sem.at[2]),
     ]
     weights = [
-        pltpu.make_async_copy(gw.at[0], gv, w_sem.at[0]),
-        pltpu.make_async_copy(uw.at[0], uv, w_sem.at[1]),
+        pltpu.make_async_copy(src, dst, w_sem.at[i])
+        for i, (src, dst) in enumerate(
+            [(sg, sgv), (su, suv), (gw.at[0], gv), (uw.at[0], uv), (dw.at[0], dv), (sd, sdv)]
+        )
     ]
-    for h in range(2):
-        for j, src in enumerate((sg, su)):
-            weights.append(pltpu.make_async_copy(
-                src.at[pl.ds(h * ll, ll)], sguv.at[h, pl.ds(j * ll, ll)], w_sem.at[2 + 2 * h + j]))
-    weights.append(pltpu.make_async_copy(dw.at[0], dv, w_sem.at[6]))
-    weights.append(pltpu.make_async_copy(sd, sdv, w_sem.at[7]))
-    for copy in inputs + weights:
+    for copy in inputs + weights[:4]:
         copy.start()
 
     barrier = pltpu.get_barrier_semaphore()
@@ -389,7 +393,7 @@
     pl.semaphore_wait(barrier, 3 + inner)
 
     def tok_copy(s, h, away):
-        block = toks.at[s, pl.ds(h * half_rows, half_rows)]
+        block = toks.at[s, span(h)]
         return remote(block, block, tok_ss.at[s, h, away], tok_rs.at[s, h],
                       {"ep": me + sign * (1 - 2 * away)})
 
@@ -398,24 +402,22 @@
                       {"ep": me + sign * (1 - 2 * away)})
 
     def mate_copy(u, j):
-        m = units[u][2]
-        return remote(part.at[u, pl.ds(0, m), pieces[j]], peer.at[u, pl.ds(0, m), pieces[j]],
+        mine = pl.ds(0, size[u])
+        return remote(part.at[u, mine, pieces[j]], peer.at[u, mine, pieces[j]],
                       d_ss.at[u, j], d_rs.at[u, j], {"sub": mate})
 
     def across_copy(u):
-        m = units[u][2]
-        return remote(xs.at[u, pl.ds(0, m)], xr.at[u, pl.ds(0, m)], x_ss.at[u], x_rs.at[u],
-                      {"sub": across})
+        mine = pl.ds(0, size[u])
+        return remote(xs.at[u, mine], xr.at[u, mine], x_ss.at[u], x_rs.at[u], {"sub": across})
 
     def hid_copy(u):
-        block = hid.at[u, core, pl.ds(0, units[u][2])]
+        block = hid.at[u, core, pl.ds(0, size[u])]
         return remote(block, block, h_ss.at[u], h_rs.at[u], {"sub": mate})
 
-    def out_copy(k, h):
-        s, where = source[k], pl.ds(h * half_rows, half_rows)
-        slot = lax.rem(me - s + n, n) - 1
-        return remote(cs.at[k - 1, where], cr.at[slot, where], c_ss.at[k - 1, h],
-                      c_rs.at[slot, h], {"ep": s})
+    def out_copy(u):
+        slot = lax.rem(me - source[u] + n, n) - 1
+        return remote(cs.at[u - 1], cr.at[slot, place(u)], c_ss.at[u - 1],
+                      c_rs.at[slot, parity[u]], {"ep": source[u]})
 
     inputs[0].wait()
     for h in range(2):
@@ -430,38 +432,42 @@
     on_inner(lambda: meta_copy(me, 1).start())
     meta_copy(me, 0).start()
 
-    def take(k, halves):
-        if 0 in halves:
-            meta_copy(source[k], 0).wait_recv()
-        for h in halves:
-            tok_copy(source[k], h, 0).wait_recv()
-
-    def forward(k, h, away):
-        s = source[k]
-        tok_copy(s, h, 0).wait_recv()
-        tok_copy(s, h, away).start()
-        if h == 0:
-            meta_copy(s, 0).wait_recv()
-            meta_copy(s, away).start()
+    def take(u):
+        def wait():
+            tok_copy(source[u], parity[u], 0).wait_recv()
+            if u % 2:
+                meta_copy(source[u], 0).wait_recv()
+
+        on_edge(wait)
+
+    def forward(u, away):
+        def send():
+            s, h = source[u], parity[u]
+            tok_copy(s, h, 0).wait_recv()
+            tok_copy(s, h, away).start()
+            if u in (1, 2, 5):
+                meta_copy(s, 0).wait_recv()
+                meta_copy(s, away).start()
+
+        on_inner(send)
 
     def project(u):
-        k, first, m = units[u]
-        block = toks.at[source[k], pl.ds(first, m)]
-        mine = pl.ds(0, m)
+        mine = pl.ds(0, size[u])
+        block = toks.at[source[u], place(u)]
         for side, dst in ((1 - core, part), (core, own)):
             cols = pl.ds(pl.multiple_of(side * hh, hh), hh)
-            dst[u, mine, pieces[0]] = dot(block[...], gv[:, cols])
-            if dst is part:
-                mate_copy(u, 0).start()
-            dst[u, mine, pieces[1]] = dot(block[...], uv[:, cols])
-            if dst is part:
-                mate_copy(u, 1).start()
-            dst[u, mine, pieces[2]] = dot(block[...], sguv[side], NT)
-            if dst is part:
-                mate_copy(u, 2).start()
+            values = (
+                lambda: dot(block[...], gv[:, cols]),
+                lambda: dot(block[...], uv[:, cols]),
+                lambda: dot(block[...], turned[side]),
+            )
+            for j, value in enumerate(values):
+                dst[u, mine, pieces[j]] = value()
+                if dst is part:
+                    mate_copy(u, j).start()
 
     def reduce(u):
-        mine = pl.ds(0, units[u][2])
+        mine = pl.ds(0, size[u])
         for j, cols in enumerate(pieces):
             mate_copy(u, j).wait_recv()
             total = own[u, mine, cols] + peer[u, mine, cols]
@@ -470,95 +476,92 @@
         across_copy(u).start()
 
     def activate(u):
-        mine = pl.ds(0, units[u][2])
+        mine = pl.ds(0, size[u])
         across_copy(u).wait_recv()
         gate, up, shared = [own[u, mine, cols] + xr[u, mine, cols].astype(F32) for cols in pieces]
         hid[u, core, mine, pl.ds(0, hh)] = (silu(gate) * up).astype(BF16)
         hid[u, core, mine, pl.ds(hh, ll)] = (silu(shared[:, :ll]) * shared[:, ll:]).astype(BF16)
         hid_copy(u).start()
 
-    def weigh(k):
-        line = metas[source[k], pl.ds(me, 1), pl.ds(0, rows)]
-        eye = (
-            lax.broadcasted_iota(jnp.int32, (rows, rows), 0)
-            == lax.broadcasted_iota(jnp.int32, (rows, rows), 1)
-        )
-        wcol[k] = jnp.sum(jnp.where(eye, line, 0.0), axis=1, keepdims=True)
-
     def finish(u):
-        k, first, m = units[u]
+        m = size[u]
         mine = pl.ds(0, m)
-        scale = wcol[k, pl.ds(first, m)]
+        line = metas[source[u], pl.ds(me, 1), pl.ds(0, rows)]
+        row = lax.broadcasted_iota(jnp.int32, (m, rows), 0) + parity[u] * half
+        eye = row == lax.broadcasted_iota(jnp.int32, (m, rows), 1)
+        scale = jnp.sum(jnp.where(eye, line, 0.0), axis=1, keepdims=True)
         hid_copy(u).wait_recv()
         routed = jnp.concatenate([hid[u, c, mine, pl.ds(0, hh)] for c in range(2)], axis=1)
         shared = jnp.concatenate([hid[u, c, mine, pl.ds(hh, ll)] for c in range(2)], axis=1)
         for c in range(width // chunk):
             cols = pl.ds(c * chunk, chunk)
             total = dot(routed, dv[:, cols]) * scale + dot(shared, sdv[:, cols])
-            if k == 0:
+            if u == 0:
                 acc[:, cols] = total
             else:
-                cs[k - 1, pl.ds(first, m), cols] = total.astype(BF16)
-        if k:
-            for h in range(first // half_rows, (first + m) // half_rows):
-                out_copy(k, h).start()
-
-    for copy in weights[:6]:
+                cs[u - 1, :, cols] = total.astype(BF16)
+        if u:
+            out_copy(u).start()
+
+    for copy in weights[:2]:
         copy.wait()
+    for side in range(2):
+        for j, src in enumerate((sgv, suv)):
+            turned[side, :, j * ll:(j + 1) * ll] = src[side * ll:(side + 1) * ll, :].T
+    for copy in weights[2:4]:
+        copy.wait()
+    for copy in weights[4:]:
+        copy.start()
     project(0)
-
-    @on_inner
-    def _():
-        forward(2, 0, 1)
-        forward(1, 0, 0)
-
-    weigh(0)
+    forward(1, 1)
+    forward(2, 0)
     reduce(0)
-
-    @on_inner
-    def _():
-        forward(2, 1, 1)
-        forward(1, 1, 0)
-
-    on_edge(lambda: take(1, (0, 1)))
+    take(1)
     project(1)
-    weigh(1)
     reduce(1)
-    on_inner(lambda: forward(3, 0, 1))
+    forward(3, 1)
+    forward(4, 0)
+    take(2)
+    project(2)
+    reduce(2)
+    forward(5, 1)
+    take(3)
+    project(3)
     activate(0)
-    on_edge(lambda: take(2, (0, 1)))
-    project(2)
-    weigh(2)
-    on_inner(lambda: forward(3, 1, 1))
-    reduce(2)
-    for copy in weights[6:]:
+    activate(1)
+    reduce(3)
+    forward(6, 1)
+    take(4)
+    project(4)
+    for copy in weights[4:]:
         copy.wait()
-    finish(0)
-    activate(1)
-    on_edge(lambda: take(3, (0,)))
-    project(3)
-    weigh(3)
-    reduce(3)
     finish(1)
-    on_edge(lambda: take(3, (1,)))
-    project(4)
+    activate(2)
     reduce(4)
-    activate(2)
+    take(5)
+    project(5)
     finish(2)
     activate(3)
+    reduce(5)
+    take(6)
+    project(6)
     finish(3)
     activate(4)
+    reduce(6)
     finish(4)
+    activate(5)
+    finish(5)
+    activate(6)
+    finish(6)
+    finish(0)
 
     for slot in range(n - 1):
         for h in range(2):
-            where = pl.ds(h * half_rows, half_rows)
-            remote(cs.at[slot, where], cr.at[slot, where], c_ss.at[slot, h], c_rs.at[slot, h],
+            remote(cs.at[0], cr.at[slot, span(h)], c_ss.at[0], c_rs.at[slot, h],
                    {"ep": me + sign}).wait_recv()
-    for k in range(1, n):
-        for h in range(2):
-            out_copy(k, h).wait_send()
-    for u in range(len(units)):
+    for u in range(len(size)):
+        if u:
+            out_copy(u).wait_send()
         for j in range(len(pieces)):
             mate_copy(u, j).wait_send()
         across_copy(u).wait_send()
@@ -570,12 +573,12 @@
     @on_inner
     def _():
         meta_copy(me, 1).wait_send()
-        for k, away in ((1, 0), (2, 1), (3, 1)):
-            meta_copy(source[k], away).wait_send()
-            for h in range(2):
-                tok_copy(source[k], h, away).wait_send()
         for h in range(2):
             tok_copy(me, h, 1).wait_send()
+        for u, away in ((1, 1), (2, 0), (3, 1), (4, 0), (5, 1), (6, 1)):
+            tok_copy(source[u], parity[u], away).wait_send()
+            if u in (1, 2, 5):
+                meta_copy(source[u], away).wait_send()
 
 
 def line_device(tokens, expert_ids, route_weights, gate_weight, up_weight, down_weight,
@@ -585,7 +588,7 @@
     top = expert_ids.shape[1]
     hidden = gate_weight.shape[2]
     local = shared_gate.shape[0]
-    both, units = hidden + local, 5
+    both, units = hidden + local, 7
     dma = pltpu.SemaphoreType.DMA
     vmem = pl.BlockSpec(memory_space=pltpu.VMEM)
     hbm = pl.BlockSpec(memory_space=pl.ANY)
@@ -602,20 +605,21 @@
             pltpu.VMEM((width, hidden), BF16),
             pltpu.VMEM((width, hidden), BF16),
             pltpu.VMEM((hidden, width), BF16),
-            pltpu.VMEM((2, local, width), BF16),
             pltpu.VMEM((local, width), BF16),
-            pltpu.VMEM((n, rows, 1), F32),
+            pltpu.VMEM((local, width), BF16),
+            pltpu.VMEM((local, width), BF16),
+            pltpu.VMEM((2, width, local), BF16),
             pltpu.VMEM((units, rows, both), F32),
             pltpu.VMEM((units, rows, both), F32),
             pltpu.VMEM((units, rows, both), F32),
             pltpu.VMEM((units, rows, both), BF16),
             pltpu.VMEM((units, rows, both), BF16),
             pltpu.VMEM((units, 2, rows, both // 2), BF16),
-            pltpu.VMEM((n - 1, rows, width), BF16),
-            dma((8,)), dma((3,)),
+            pltpu.VMEM((units - 1, rows // 2, width), BF16),
+            dma((6,)), dma((3,)),
             dma((n, 2, 2)), dma((n, 2)), dma((n, 2)), dma((n,)),
             dma((units, 3)), dma((units, 3)), dma((units,)), dma((units,)),
-            dma((units,)), dma((units,)), dma((n - 1, 2)), dma((n - 1, 2)),
+            dma((units,)), dma((units,)), dma((units - 1,)), dma((n - 1, 2)),
         ],
         compiler_params=pltpu.CompilerParams(collective_id=0, has_side_effects=True),
     )(tokens, expert_ids.T, route_weights.T, gate_weight, up_weight, down_weight,

time: 55.1 us -> 49.7 us (0.902)
  Pallas kernels: 54.2 us -> 48.8 us
    pallas_call x1, Pallas kernels: 54.2 us -> 48.8 us  [line_device(): pl.pallas_call(functools.partial(line_kernel, n, ns, top), out_shape=(plt...]
where the time goes in v2:
time: 49.7 us; the launch traced here: 49.6 us
  Pallas kernels  48.8 us (98%)
  other arithmetic  0.79 us (2%)
    pallas_call x1, Pallas kernels, line_device(): pl.pallas_call(functools.partial(line_kernel, n, ns, top), out_shape=(plt...  48.8 us

profile of v2, /device:TPU:0, one launch (start us, length us, event | category | flops | bytes accessed | tf_op | source)
XLA Modules:
  0.0 49.6 jit_solution(4173740647769163102)
XLA Ops:
  0.0 48.8 %shard_map.91 = (f32[64,1792]{1,0:T(8,128)S(1)}, bf16[3,64,1792]{2,1,0:T(8,128)(2,1)S(1)}) custom-call(bf16[64,1792]{1,0:T(8,128)(2,1)} %tok.1, s32[2,64]{1,0:T(2,128)} %bitcast.11, f32[2,64]{1,0:T(2,128)} %bitcast.12, bf16[1,1792,1024]{2,1,0:T(8,128)(2,1)} %gw.1, bf16[1,1792,1024]{2,1,0:T(8,128)(2,1)} %uw.1, bf16[1,1024,1792]{2,1,0:T(8,128)(2,1)} %dw.1, ...), custom_call_target="tpu_custom_call" | custom-call | tf_op jit(solution)/shard_map/pallas_call | solution.py:595
  48.8 0.8 %fusion = bf16[64,1792]{1,0:T(8,128)(2,1)} fusion(f32[64,1792]{1,0:T(8,128)S(1)} %get-tuple-element.7, bf16[3,64,1792]{2,1,0:T(8,128)(2,1)S(1)} %get-tuple-element.8), kind=kLoop, calls=%fused_computation.1 | loop fusion | flops 802816 | bytes 1376256 | tf_op jit(solution)/shard_map/convert_element_type | solution.py:629

commit v3 on v2

--- a/solution.py
+++ b/solution.py
@@ -332,9 +332,9 @@
 
 def line_kernel(
     n, ns, top, tok, ids, rw, gw, uw, dw, sg, su, sd, acc, cr,
-    toks, metas, idv, rwv, gv, uv, dv, sgv, suv, sdv, turned, part, peer, own, xs, xr, hid, cs,
+    toks, metas, idv, rwv, gv, uv, dv, sgv, suv, sdv, turned, part, peer, own, xs, xr, hid, cs, hold, joint,
     w_sem, in_sem, tok_ss, tok_rs, meta_ss, meta_rs, d_ss, d_rs, x_ss, x_rs, h_ss, h_rs,
-    c_ss, c_rs,
+    c_ss, c_rs, j_rs,
 ):
     me, mq = lax.axis_index("ep"), lax.axis_index("sub")
     rows, width = tok.shape
@@ -346,14 +346,16 @@
     across = lax.rem(mq + 2, ns)
     sign = 1 - 2 * (me // 2)
     inner = ((me + 1) // 2) % 2
-    steps = [0, 1, 1 - 2 * inner, 2 - inner, 2 - 3 * inner, 3 - inner, 3 - inner]
+    steps = [0, 1, 1, 2, 2, 3 - 4 * inner, 3 - 4 * inner]
     source = [me + sign * step for step in steps]
-    parity = [0, 0, 1 - inner, inner, 1, 0, 1]
+    parity = [0, 0, 1, 0, 1, 0, 1]
     size = [rows] + [half] * 6
+    left = width // 2 // 128 * 128
+    sides = [pl.ds(0, left), pl.ds(left, width - left)]
     pieces = [pl.ds(0, hh), pl.ds(hh, hh), pl.ds(2 * hh, 2 * ll)]
 
     def span(h):
-        return pl.ds(h * half if isinstance(h, int) else pl.multiple_of(h * half, half), half)
+        return pl.ds(h * half, half)
 
     def place(u):
         return pl.ds(0, rows) if u == 0 else span(parity[u])
@@ -381,7 +383,7 @@
             [(sg, sgv), (su, suv), (gw.at[0], gv), (uw.at[0], uv), (dw.at[0], dv), (sd, sdv)]
         )
     ]
-    for copy in inputs + weights[:4]:
+    for copy in inputs:
         copy.start()
 
     barrier = pltpu.get_barrier_semaphore()
@@ -390,7 +392,6 @@
         barrier, inc=1, device_id={"ep": me - sign}, device_id_type=MESH))
     pl.semaphore_signal(barrier, inc=1, device_id={"sub": mate}, device_id_type=MESH)
     pl.semaphore_signal(barrier, inc=1, device_id={"sub": across}, device_id_type=MESH)
-    pl.semaphore_wait(barrier, 3 + inner)
 
     def tok_copy(s, h, away):
         block = toks.at[s, span(h)]
@@ -401,10 +402,9 @@
         return remote(metas.at[s], metas.at[s], meta_ss.at[s, away], meta_rs.at[s],
                       {"ep": me + sign * (1 - 2 * away)})
 
-    def mate_copy(u, j):
+    def mate_copy(u):
         mine = pl.ds(0, size[u])
-        return remote(part.at[u, mine, pieces[j]], peer.at[u, mine, pieces[j]],
-                      d_ss.at[u, j], d_rs.at[u, j], {"sub": mate})
+        return remote(part.at[u, mine], peer.at[u, mine], d_ss.at[u], d_rs.at[u], {"sub": mate})
 
     def across_copy(u):
         mine = pl.ds(0, size[u])
@@ -414,23 +414,34 @@
         block = hid.at[u, core, pl.ds(0, size[u])]
         return remote(block, block, h_ss.at[u], h_rs.at[u], {"sub": mate})
 
-    def out_copy(u):
+    def out_copy(u, c):
         slot = lax.rem(me - source[u] + n, n) - 1
-        return remote(cs.at[u - 1], cr.at[slot, place(u)], c_ss.at[u - 1],
-                      c_rs.at[slot, parity[u]], {"ep": source[u]})
-
-    inputs[0].wait()
-    for h in range(2):
-        on_inner(lambda h=h: tok_copy(me, h, 1).start())
-        tok_copy(me, h, 0).start()
+        return remote(cs.at[u - 1, :, sides[c]], cr.at[slot, place(u), sides[c]],
+                      c_ss.at[u - 1, c], c_rs.at[slot, parity[u], c], {"ep": source[u]})
+
+    def far_copy(u, c):
+        return remote(cs.at[u - 1, :, sides[c]], joint.at[u - 5, :, sides[c]],
+                      c_ss.at[u - 1, c], j_rs.at[u - 5, c], {"ep": me + sign})
+
     inputs[1].wait()
     inputs[2].wait()
     metas[me] = jnp.zeros(metas.shape[1:], F32)
     for e in range(n):
         metas[me, e:e + 1, :rows] = jnp.sum(
             jnp.where(idv[...] == e, rwv[...], 0.0), axis=0, keepdims=True)
+    inputs[0].wait()
+    pl.semaphore_wait(barrier, 3 + inner)
+    for h in range(2):
+        on_inner(lambda h=h: tok_copy(me, h, 1).start())
+        tok_copy(me, h, 0).start()
     on_inner(lambda: meta_copy(me, 1).start())
     meta_copy(me, 0).start()
+    for copy in weights:
+        copy.start()
+
+    @on_edge
+    def _():
+        cr[lax.rem(source[5] - me + n, n) - 1] = jnp.zeros((rows, width), BF16)
 
     def take(u):
         def wait():
@@ -445,34 +456,31 @@
             s, h = source[u], parity[u]
             tok_copy(s, h, 0).wait_recv()
             tok_copy(s, h, away).start()
-            if u in (1, 2, 5):
+            if u % 2:
                 meta_copy(s, 0).wait_recv()
                 meta_copy(s, away).start()
 
         on_inner(send)
 
-    def project(u):
-        mine = pl.ds(0, size[u])
-        block = toks.at[source[u], place(u)]
+    def project(*group):
+        block = jnp.concatenate([toks[source[v], place(v)] for v in group], axis=0)
         for side, dst in ((1 - core, part), (core, own)):
             cols = pl.ds(pl.multiple_of(side * hh, hh), hh)
-            values = (
-                lambda: dot(block[...], gv[:, cols]),
-                lambda: dot(block[...], uv[:, cols]),
-                lambda: dot(block[...], turned[side]),
-            )
-            for j, value in enumerate(values):
-                dst[u, mine, pieces[j]] = value()
-                if dst is part:
-                    mate_copy(u, j).start()
+            for j, matrix in enumerate((gv.at[:, cols], uv.at[:, cols], turned.at[side])):
+                result, first = dot(block, matrix[...]), 0
+                for v in group:
+                    dst[v, pl.ds(0, size[v]), pieces[j]] = result[first:first + size[v]]
+                    first += size[v]
+            if dst is part:
+                for v in group:
+                    mate_copy(v).start()
 
     def reduce(u):
         mine = pl.ds(0, size[u])
-        for j, cols in enumerate(pieces):
-            mate_copy(u, j).wait_recv()
-            total = own[u, mine, cols] + peer[u, mine, cols]
-            own[u, mine, cols] = total
-            xs[u, mine, cols] = total.astype(BF16)
+        mate_copy(u).wait_recv()
+        total = own[u, mine] + peer[u, mine]
+        own[u, mine] = total
+        xs[u, mine] = total.astype(BF16)
         across_copy(u).start()
 
     def activate(u):
@@ -483,25 +491,58 @@
         hid[u, core, mine, pl.ds(hh, ll)] = (silu(shared[:, :ll]) * shared[:, ll:]).astype(BF16)
         hid_copy(u).start()
 
-    def finish(u):
-        m = size[u]
-        mine = pl.ds(0, m)
-        line = metas[source[u], pl.ds(me, 1), pl.ds(0, rows)]
-        row = lax.broadcasted_iota(jnp.int32, (m, rows), 0) + parity[u] * half
-        eye = row == lax.broadcasted_iota(jnp.int32, (m, rows), 1)
-        scale = jnp.sum(jnp.where(eye, line, 0.0), axis=1, keepdims=True)
-        hid_copy(u).wait_recv()
-        routed = jnp.concatenate([hid[u, c, mine, pl.ds(0, hh)] for c in range(2)], axis=1)
-        shared = jnp.concatenate([hid[u, c, mine, pl.ds(hh, ll)] for c in range(2)], axis=1)
+    def finish(*group):
+        scales = []
+        for v in group:
+            m = size[v]
+            line = metas[source[v], pl.ds(me, 1), pl.ds(0, rows)]
+            row = lax.broadcasted_iota(jnp.int32, (m, rows), 0) + parity[v] * half
+            eye = row == lax.broadcasted_iota(jnp.int32, (m, rows), 1)
+            scales.append(jnp.sum(jnp.where(eye, line, 0.0), axis=1, keepdims=True))
+        scale = jnp.concatenate(scales, axis=0)
+        for v in group:
+            hid_copy(v).wait_recv()
+        routed, shared = [
+            jnp.concatenate([
+                jnp.concatenate([hid[v, c, pl.ds(0, size[v]), cols] for c in range(2)], axis=1)
+                for v in group], axis=0)
+            for cols in (pl.ds(0, hh), pl.ds(hh, ll))
+        ]
         for c in range(width // chunk):
             cols = pl.ds(c * chunk, chunk)
-            total = dot(routed, dv[:, cols]) * scale + dot(shared, sdv[:, cols])
-            if u == 0:
-                acc[:, cols] = total
-            else:
-                cs[u - 1, :, cols] = total.astype(BF16)
-        if u:
-            out_copy(u).start()
+            total, first = dot(routed, dv[:, cols]) * scale + dot(shared, sdv[:, cols]), 0
+            for v in group:
+                value = total[first:first + size[v]]
+                first += size[v]
+                if v == 0:
+                    acc[:, cols] = value
+                    continue
+                cs[v - 1, :, cols] = value.astype(BF16)
+                if v in (3, 4):
+                    hold[v - 3, :, cols] = value
+
+        def ship(v, copy):
+            for c in range(2):
+                copy(v, c).start()
+
+        for v in group:
+            if v in (1, 2):
+                ship(v, out_copy)
+            elif v in (3, 4):
+                on_edge(lambda: ship(v, out_copy))
+            elif v:
+                on_edge(lambda: ship(v, far_copy))
+                on_inner(lambda: ship(v, out_copy))
+
+    def join(u, c):
+        def add():
+            far_copy(u + 2, c).wait_recv()
+            cs[u - 1, :, sides[c]] = (
+                hold[u - 3, :, sides[c]] + joint[u - 3, :, sides[c]].astype(F32)
+            ).astype(BF16)
+            out_copy(u, c).start()
+
+        on_inner(add)
 
     for copy in weights[:2]:
         copy.wait()
@@ -510,27 +551,22 @@
             turned[side, :, j * ll:(j + 1) * ll] = src[side * ll:(side + 1) * ll, :].T
     for copy in weights[2:4]:
         copy.wait()
-    for copy in weights[4:]:
-        copy.start()
-    project(0)
     forward(1, 1)
-    forward(2, 0)
-    reduce(0)
+    forward(5, 0)
     take(1)
-    project(1)
+    project(1, 0)
     reduce(1)
-    forward(3, 1)
-    forward(4, 0)
+    forward(2, 1)
+    forward(6, 0)
     take(2)
     project(2)
     reduce(2)
-    forward(5, 1)
+    forward(3, 1)
     take(3)
     project(3)
-    activate(0)
     activate(1)
     reduce(3)
-    forward(6, 1)
+    forward(4, 1)
     take(4)
     project(4)
     for copy in weights[4:]:
@@ -548,22 +584,34 @@
     finish(3)
     activate(4)
     reduce(6)
+    reduce(0)
     finish(4)
     activate(5)
     finish(5)
     activate(6)
+    activate(0)
     finish(6)
     finish(0)
 
-    for slot in range(n - 1):
+    for u in (3, 4):
+        for c in range(2):
+            join(u, c)
+
+    def landed(k):
+        slot = lax.rem(source[k] - me + n, n) - 1
         for h in range(2):
-            remote(cs.at[0], cr.at[slot, span(h)], c_ss.at[0], c_rs.at[slot, h],
-                   {"ep": me + sign}).wait_recv()
+            for c in range(2):
+                remote(cs.at[0, :, sides[c]], cr.at[slot, span(h), sides[c]], c_ss.at[0, c],
+                       c_rs.at[slot, h, c], {"ep": me + sign}).wait_recv()
+
+    landed(1)
+    landed(3)
+    on_inner(lambda: landed(5))
     for u in range(len(size)):
         if u:
-            out_copy(u).wait_send()
-        for j in range(len(pieces)):
-            mate_copy(u, j).wait_send()
+            for c in range(2):
+                out_copy(u, c).wait_send()
+        mate_copy(u).wait_send()
         across_copy(u).wait_send()
         hid_copy(u).wait_send()
     for h in range(2):
@@ -575,9 +623,9 @@
         meta_copy(me, 1).wait_send()
         for h in range(2):
             tok_copy(me, h, 1).wait_send()
-        for u, away in ((1, 1), (2, 0), (3, 1), (4, 0), (5, 1), (6, 1)):
+        for u, away in ((1, 1), (2, 1), (3, 1), (4, 1), (5, 0), (6, 0)):
             tok_copy(source[u], parity[u], away).wait_send()
-            if u in (1, 2, 5):
+            if u % 2:
                 meta_copy(source[u], away).wait_send()
 
 
@@ -616,10 +664,12 @@
             pltpu.VMEM((units, rows, both), BF16),
             pltpu.VMEM((units, 2, rows, both // 2), BF16),
             pltpu.VMEM((units - 1, rows // 2, width), BF16),
+            pltpu.VMEM((2, rows // 2, width), F32),
+            pltpu.VMEM((2, rows // 2, width), BF16),
             dma((6,)), dma((3,)),
             dma((n, 2, 2)), dma((n, 2)), dma((n, 2)), dma((n,)),
-            dma((units, 3)), dma((units, 3)), dma((units,)), dma((units,)),
-            dma((units,)), dma((units,)), dma((units - 1,)), dma((n - 1, 2)),
+            dma((units,)), dma((units,)), dma((units,)), dma((units,)),
+            dma((units,)), dma((units,)), dma((units - 1, 2)), dma((n - 1, 2, 2)), dma((2, 2)),
         ],
         compiler_params=pltpu.CompilerParams(collective_id=0, has_side_effects=True),
     )(tokens, expert_ids.T, route_weights.T, gate_weight, up_weight, down_weight,

time: 49.7 us -> 45.8 us (0.922)
  Pallas kernels: 48.8 us -> 44.9 us
    pallas_call x1, Pallas kernels: 48.8 us -> 44.9 us  [line_device(): pl.pallas_call(functools.partial(line_kernel, n, ns, top), out_shape=(plt...]
where the time goes in v3:
time: 45.8 us; the launch traced here: 45.7 us
  Pallas kernels  44.9 us (98%)
  other arithmetic  0.79 us (2%)
    pallas_call x1, Pallas kernels, line_device(): pl.pallas_call(functools.partial(line_kernel, n, ns, top), out_shape=(plt...  44.9 us

profile of v3, /device:TPU:0, one launch (start us, length us, event | category | flops | bytes accessed | tf_op | source)
XLA Modules:
  0.0 45.7 jit_solution(17432714297462936426)
XLA Ops:
  0.0 44.9 %shard_map.91 = (f32[64,1792]{1,0:T(8,128)S(1)}, bf16[3,64,1792]{2,1,0:T(8,128)(2,1)S(1)}) custom-call(bf16[64,1792]{1,0:T(8,128)(2,1)} %tok.1, s32[2,64]{1,0:T(2,128)} %bitcast.11, f32[2,64]{1,0:T(2,128)} %bitcast.12, bf16[1,1792,1024]{2,1,0:T(8,128)(2,1)} %gw.1, bf16[1,1792,1024]{2,1,0:T(8,128)(2,1)} %uw.1, bf16[1,1024,1792]{2,1,0:T(8,128)(2,1)} %dw.1, ...), custom_call_target="tpu_custom_call" | custom-call | tf_op jit(solution)/shard_map/pallas_call | solution.py:643
  44.9 0.8 %fusion = bf16[64,1792]{1,0:T(8,128)(2,1)} fusion(f32[64,1792]{1,0:T(8,128)S(1)} %get-tuple-element.7, bf16[3,64,1792]{2,1,0:T(8,128)(2,1)S(1)} %get-tuple-element.8), kind=kLoop, calls=%fused_computation.1 | loop fusion | flops 802816 | bytes 1376256 | tf_op jit(solution)/shard_map/convert_element_type | solution.py:679

commit v4 on v3

--- a/solution.py
+++ b/solution.py
@@ -350,7 +350,7 @@
     source = [me + sign * step for step in steps]
     parity = [0, 0, 1, 0, 1, 0, 1]
     size = [rows] + [half] * 6
-    left = width // 2 // 128 * 128
+    left = width // 2 // chunk * chunk
     sides = [pl.ds(0, left), pl.ds(left, width - left)]
     pieces = [pl.ds(0, hh), pl.ds(hh, hh), pl.ds(2 * hh, 2 * ll)]
 
@@ -508,6 +508,16 @@
                 for v in group], axis=0)
             for cols in (pl.ds(0, hh), pl.ds(hh, ll))
         ]
+        def ship(c):
+            for v in group:
+                if v in (1, 2):
+                    out_copy(v, c).start()
+                elif v in (3, 4):
+                    on_edge(lambda: out_copy(v, c).start())
+                elif v:
+                    on_edge(lambda: far_copy(v, c).start())
+                    on_inner(lambda: out_copy(v, c).start())
+
         for c in range(width // chunk):
             cols = pl.ds(c * chunk, chunk)
             total, first = dot(routed, dv[:, cols]) * scale + dot(shared, sdv[:, cols]), 0
@@ -520,19 +530,8 @@
                 cs[v - 1, :, cols] = value.astype(BF16)
                 if v in (3, 4):
                     hold[v - 3, :, cols] = value
-
-        def ship(v, copy):
-            for c in range(2):
-                copy(v, c).start()
-
-        for v in group:
-            if v in (1, 2):
-                ship(v, out_copy)
-            elif v in (3, 4):
-                on_edge(lambda: ship(v, out_copy))
-            elif v:
-                on_edge(lambda: ship(v, far_copy))
-                on_inner(lambda: ship(v, out_copy))
+            if (c + 1) * chunk in (left, width):
+                ship((c + 1) * chunk // width)
 
     def join(u, c):
         def add():
@@ -589,13 +588,12 @@
     activate(5)
     finish(5)
     activate(6)
-    activate(0)
     finish(6)
-    finish(0)
-
     for u in (3, 4):
         for c in range(2):
             join(u, c)
+    activate(0)
+    finish(0)
 
     def landed(k):
         slot = lax.rem(source[k] - me + n, n) - 1

time: 45.8 us -> 44.7 us (0.976)
  Pallas kernels: 44.9 us -> 43.8 us
    pallas_call x1, Pallas kernels: 44.9 us -> 43.8 us  [line_device(): pl.pallas_call(functools.partial(line_kernel, n, ns, top), out_shape=(plt...]
where the time goes in v4:
time: 44.7 us; the launch traced here: 44.6 us
  Pallas kernels  43.8 us (98%)
  other arithmetic  0.79 us (2%)
    pallas_call x1, Pallas kernels, line_device(): pl.pallas_call(functools.partial(line_kernel, n, ns, top), out_shape=(plt...  43.8 us

profile of v4, /device:TPU:0, one launch (start us, length us, event | category | flops | bytes accessed | tf_op | source)
XLA Modules:
  0.0 44.6 jit_solution(15716174189540444157)
XLA Ops:
  0.0 43.8 %shard_map.91 = (f32[64,1792]{1,0:T(8,128)S(1)}, bf16[3,64,1792]{2,1,0:T(8,128)(2,1)S(1)}) custom-call(bf16[64,1792]{1,0:T(8,128)(2,1)} %tok.1, s32[2,64]{1,0:T(2,128)} %bitcast.11, f32[2,64]{1,0:T(2,128)} %bitcast.12, bf16[1,1792,1024]{2,1,0:T(8,128)(2,1)} %gw.1, bf16[1,1792,1024]{2,1,0:T(8,128)(2,1)} %uw.1, bf16[1,1024,1792]{2,1,0:T(8,128)(2,1)} %dw.1, ...), custom_call_target="tpu_custom_call" | custom-call | tf_op jit(solution)/shard_map/pallas_call | solution.py:641
  43.8 0.8 %fusion = bf16[64,1792]{1,0:T(8,128)(2,1)} fusion(f32[64,1792]{1,0:T(8,128)S(1)} %get-tuple-element.7, bf16[3,64,1792]{2,1,0:T(8,128)(2,1)S(1)} %get-tuple-element.8), kind=kLoop, calls=%fused_computation.1 | loop fusion | flops 802816 | bytes 1376256 | tf_op jit(solution)/shard_map/convert_element_type | solution.py:677
